TPU v7x, 32 devices: a whole 2x2x4 slice. The times are simulated.
32 devices in a mesh: fsdp: 4 (over y, x), seq: 8 (over z, core).
Axes of the slice: x: 2, y: 2, z: 4, core: 2. Of those that a mesh axis runs over, the one named last changes fastest.
Arguments:
- images: bfloat16 [32, 1024, 1152], P('fsdp', 'seq'), may hold values from -8 to 8
- lengths: int32 [32], P('fsdp'), may hold values from 256 to 1024
- ln1_gain: bfloat16 [1152], P('fsdp'), may hold values from 0.099609375 to 1.8984375
- ln1_bias: bfloat16 [1152], P('fsdp'), may hold values from -3 to 3
- w_qkv: bfloat16 [1152, 3456], P('fsdp'), may hold values from -1 to 1
- qv_bias: bfloat16 [2, 1152], P(None, 'fsdp'), may hold values from -3 to 3
- w_out: bfloat16 [1152, 1152], P('fsdp'), may hold values from -0.75 to 0.75
- out_bias: bfloat16 [1152], P('fsdp'), may hold values from -3 to 3
- ln2_gain: bfloat16 [1152], P('fsdp'), may hold values from 0.099609375 to 1.8984375
- ln2_bias: bfloat16 [1152], P('fsdp'), may hold values from -3 to 3
- w_up: bfloat16 [1152, 4304], P('fsdp'), may hold values from -0.1875 to 0.1875
- up_bias: bfloat16 [4304], P('fsdp'), may hold values from -3 to 3
- w_down: bfloat16 [4304, 1152], P(None, 'fsdp'), may hold values from -0.09375 to 0.09375
- down_bias: bfloat16 [1152], P('fsdp'), may hold values from -3 to 3
- cotangent: bfloat16 [32, 1024, 1152], P('fsdp', 'seq'), may hold values from -6 to 6
Outputs:
- layer_out: bfloat16 [32, 1024, 1152], P('fsdp', 'seq')
- grad_images: bfloat16 [32, 1024, 1152], P('fsdp', 'seq')
- grad_ln1_gain: float32 [1152], P('fsdp')
- grad_ln1_bias: float32 [1152], P('fsdp')
- grad_w_qkv: float32 [1152, 3456], P('fsdp')
- grad_qv_bias: float32 [2, 1152], P(None, 'fsdp')
- grad_w_out: float32 [1152, 1152], P('fsdp')
- grad_out_bias: float32 [1152], P('fsdp')
- grad_ln2_gain: float32 [1152], P('fsdp')
- grad_ln2_bias: float32 [1152], P('fsdp')
- grad_w_up: float32 [1152, 4304], P('fsdp')
- grad_up_bias: float32 [4304], P('fsdp')
- grad_w_down: float32 [4304, 1152], P(None, 'fsdp')
- grad_down_bias: float32 [1152], P('fsdp')
All inputs are finite; a program needn't handle non-finite values.
Results may differ from a plain program's by a relative error of at most 0.017.
Values may be sent and summed in bfloat16 or wider, within the bound.
A program may use at most 256 MiB of HBM per device.

v0:
```python
import jax
import jax.numpy as jnp
from jax import lax
from jax.sharding import PartitionSpec as P

H = 16
HD = 72


epsilon = 1e-06
wide_block = 1024


def for_sending(shard):

    def short(part):
        return part.astype(jnp.bfloat16) if part.dtype == jnp.float32 else part

    return jax.tree.map(short, shard)


def normalize(field, gain_vec, bias_vec):
    center_mean = jnp.mean(field, -1, keepdims=True)
    centered = field - center_mean
    variance = jnp.mean(centered * centered, -1, keepdims=True)
    return centered * lax.rsqrt(variance + epsilon) * gain_vec + bias_vec


def gelu_tanh(field):
    return jax.nn.gelu(field, approximate=True)


def attend_item(queries, keys_all, values, length_one):
    length_all = keys_all.shape[1]
    block_rows = min(wide_block, length_all)
    visible = (jnp.arange(length_all) < length_one)[None, :]
    pieces = []
    log_sums = []
    for offset in range(0, length_all, block_rows):
        scores = jnp.einsum(
            "dq,dk->qk",
            queries[:, offset : offset + block_rows],
            keys_all,
            preferred_element_type=jnp.float32,
        )
        scores = jnp.where(visible, scores, -1e30)
        row_max = jnp.max(scores, -1, keepdims=True)
        exponents = jnp.exp(scores - row_max)
        denominator = jnp.sum(exponents, -1, keepdims=True)
        softmax_low = (exponents / denominator).astype(jnp.bfloat16)
        pieces.append(
            jnp.einsum("qk,dk->dq", softmax_low, values, preferred_element_type=jnp.float32)
        )
        log_sums.append(row_max[:, 0] + jnp.log(denominator[:, 0]))
    return (jnp.concatenate(pieces, 1).astype(jnp.bfloat16), jnp.concatenate(log_sums, 0))


def attend_back(queries, keys_all, values, length_one, log_sum, grad_mixed):
    length_all = keys_all.shape[1]
    block_rows = min(wide_block, length_all)
    visible = (jnp.arange(length_all) < length_one)[None, :]
    grad_keys = jnp.zeros(keys_all.shape, jnp.float32)
    grad_values = jnp.zeros(values.shape, jnp.float32)
    grad_pieces = []
    for offset in range(0, length_all, block_rows):
        query_rows = queries[:, offset : offset + block_rows]
        grad_rows = grad_mixed[:, offset : offset + block_rows]
        scores = jnp.einsum("dq,dk->qk", query_rows, keys_all, preferred_element_type=jnp.float32)
        scores = jnp.where(visible, scores, -1e30)
        softmax_out = jnp.exp(scores - log_sum[offset : offset + block_rows, None])
        grad_soft = jnp.einsum("dq,dk->qk", grad_rows, values, preferred_element_type=jnp.float32)
        row_dot = jnp.sum(softmax_out * grad_soft, -1, keepdims=True)
        grad_scores = (softmax_out * (grad_soft - row_dot)).astype(jnp.bfloat16)
        grad_pieces.append(
            jnp.einsum("qk,dk->dq", grad_scores, keys_all, preferred_element_type=jnp.float32)
        )
        grad_keys = grad_keys + jnp.einsum(
            "qk,dq->dk", grad_scores, query_rows, preferred_element_type=jnp.float32
        )
        grad_values = grad_values + jnp.einsum(
            "qk,dq->dk",
            softmax_out.astype(jnp.bfloat16),
            grad_rows,
            preferred_element_type=jnp.float32,
        )
    return (
        jnp.concatenate(grad_pieces, 1).astype(jnp.bfloat16),
        grad_keys.astype(jnp.bfloat16),
        grad_values.astype(jnp.bfloat16),
    )


def on_device(
    images,
    lengths,
    ln1_gain,
    ln1_bias,
    w_qkv,
    qv_bias,
    w_out,
    out_bias,
    ln2_gain,
    ln2_bias,
    w_up,
    up_bias,
    w_down,
    down_bias,
    cotangent,
):
    image_count, token_count, width_all = images.shape
    head_scale = HD ** (-0.5)
    gain_first, bias_first, qkv_full, qv_full, out_full, outb_full = (
        lax.all_gather(ln1_gain, "fsdp", axis=0, tiled=True),
        lax.all_gather(ln1_bias, "fsdp", axis=0, tiled=True),
        lax.all_gather(w_qkv, "fsdp", axis=0, tiled=True),
        lax.all_gather(qv_bias, "fsdp", axis=1, tiled=True),
        lax.all_gather(w_out, "fsdp", axis=0, tiled=True),
        lax.all_gather(out_bias, "fsdp", axis=0, tiled=True),
    )
    inputs_all = images.astype(jnp.float32)
    normed_first, norm_first_back = jax.vjp(
        normalize, inputs_all, gain_first.astype(jnp.float32), bias_first.astype(jnp.float32)
    )
    normed_attn = normed_first.astype(jnp.bfloat16)
    qkv_split = qkv_full.reshape(width_all, 3, H, HD)
    projected = jnp.einsum(
        "itd,dahe->ahiet", normed_attn, qkv_split, preferred_element_type=jnp.float32
    )
    shift_pair = qv_full.astype(jnp.float32).reshape(2, H, HD)
    queries = (projected[0] + shift_pair[0][:, None, :, None]) * head_scale
    values = projected[2] + shift_pair[1][:, None, :, None]
    stacked = jnp.stack([queries, projected[1], values]).astype(jnp.bfloat16)
    head_view = lax.all_to_all(stacked, "seq", split_axis=1, concat_axis=4, tiled=True)
    local_heads = head_view.shape[1]
    item_count = local_heads * image_count
    query_items = head_view[0].reshape(item_count, HD, -1)
    key_items = head_view[1].reshape(item_count, HD, -1)
    value_items = head_view[2].reshape(item_count, HD, -1)
    item_lengths = jnp.tile(lengths, local_heads)
    mixed_items, log_sums = lax.map(
        lambda packed: attend_item(*packed), (query_items, key_items, value_items, item_lengths)
    )
    mixed_tokens = lax.all_to_all(
        for_sending(mixed_items.reshape(local_heads, image_count, HD, -1)),
        "seq",
        split_axis=3,
        concat_axis=0,
        tiled=True,
    )
    out_split = out_full.reshape(H, HD, width_all)
    residual = (
        inputs_all
        + jnp.einsum("hiet,hed->itd", mixed_tokens, out_split, preferred_element_type=jnp.float32)
        + outb_full.astype(jnp.float32)
    )
    gain_second, bias_second, up_full, upb_full, down_full, downb_full = (
        lax.all_gather(ln2_gain, "fsdp", axis=0, tiled=True),
        lax.all_gather(ln2_bias, "fsdp", axis=0, tiled=True),
        lax.all_gather(w_up, "fsdp", axis=0, tiled=True),
        lax.all_gather(up_bias, "fsdp", axis=0, tiled=True),
        lax.all_gather(w_down, "fsdp", axis=1, tiled=True),
        lax.all_gather(down_bias, "fsdp", axis=0, tiled=True),
    )
    normed_second, norm_second_back = jax.vjp(
        normalize, residual, gain_second.astype(jnp.float32), bias_second.astype(jnp.float32)
    )
    normed_mlp = normed_second.astype(jnp.bfloat16)
    pre_act = jnp.einsum(
        "itd,df->itf", normed_mlp, up_full, preferred_element_type=jnp.float32
    ) + upb_full.astype(jnp.float32)
    activation, gelu_back = jax.vjp(gelu_tanh, pre_act)
    activation = activation.astype(jnp.bfloat16)
    output_all = (
        residual
        + jnp.einsum("itf,fd->itd", activation, down_full, preferred_element_type=jnp.float32)
        + downb_full.astype(jnp.float32)
    )
    layer_out = output_all.astype(jnp.bfloat16)
    qkv_back, out_back = (
        lax.all_gather(w_qkv, "fsdp", axis=0, tiled=True),
        lax.all_gather(w_out, "fsdp", axis=0, tiled=True),
    )
    up_back, down_back = (
        lax.all_gather(w_up, "fsdp", axis=0, tiled=True),
        lax.all_gather(w_down, "fsdp", axis=1, tiled=True),
    )
    grad_down = jnp.einsum("itf,itd->fd", activation, cotangent, preferred_element_type=jnp.float32)
    grad_downb = jnp.sum(cotangent, axis=(0, 1), dtype=jnp.float32)
    grad_act = jnp.einsum("itd,fd->itf", cotangent, down_back, preferred_element_type=jnp.float32)
    (grad_pre,) = gelu_back(grad_act)
    grad_pre = grad_pre.astype(jnp.bfloat16)
    grad_up = jnp.einsum("itd,itf->df", normed_mlp, grad_pre, preferred_element_type=jnp.float32)
    grad_upb = jnp.sum(grad_pre, axis=(0, 1), dtype=jnp.float32)
    grad_normed_mlp = jnp.einsum(
        "itf,df->itd", grad_pre, up_back, preferred_element_type=jnp.float32
    )
    grad_resid_norm, grad_gain_second, grad_bias_second = norm_second_back(grad_normed_mlp)
    grad_residual = cotangent.astype(jnp.float32) + grad_resid_norm
    grad_branch = grad_residual.astype(jnp.bfloat16)
    grad_outw = jnp.einsum(
        "hiet,itd->hed", mixed_tokens, grad_branch, preferred_element_type=jnp.float32
    ).reshape(width_all, width_all)
    grad_outb = jnp.sum(grad_branch, axis=(0, 1), dtype=jnp.float32)
    out_back_split = out_back.reshape(H, HD, width_all)
    grad_mixed = jnp.einsum(
        "itd,hed->hiet", grad_branch, out_back_split, preferred_element_type=jnp.float32
    ).astype(jnp.bfloat16)
    grad_head_view = lax.all_to_all(grad_mixed, "seq", split_axis=0, concat_axis=3, tiled=True)
    grad_items = grad_head_view.reshape(item_count, HD, -1)
    grad_q, grad_k, grad_v = lax.map(
        lambda packed: attend_back(*packed),
        (query_items, key_items, value_items, item_lengths, log_sums, grad_items),
    )
    grad_stack = jnp.stack([grad_q, grad_k, grad_v]).reshape(3, local_heads, image_count, HD, -1)
    grad_projected = lax.all_to_all(
        for_sending(grad_stack), "seq", split_axis=4, concat_axis=1, tiled=True
    ).astype(grad_stack.dtype)
    column_scales = jnp.array([head_scale, 1.0, 1.0], jnp.float32)
    grad_qkv = (
        jnp.einsum(
            "itd,ahiet->dahe", normed_attn, grad_projected, preferred_element_type=jnp.float32
        )
        * column_scales[None, :, None, None]
    ).reshape(width_all, 3 * width_all)
    shift_sums = jnp.sum(grad_projected, axis=(2, 4), dtype=jnp.float32)
    grad_qvb = jnp.stack([shift_sums[0] * head_scale, shift_sums[2]]).reshape(2, width_all)
    qkv_back_split = qkv_back.reshape(width_all, 3, H, HD)
    grad_normed_attn = head_scale * jnp.einsum(
        "hiet,dhe->itd", grad_projected[0], qkv_back_split[:, 0], preferred_element_type=jnp.float32
    )
    grad_normed_attn = grad_normed_attn + jnp.einsum(
        "ahiet,dahe->itd",
        grad_projected[1:],
        qkv_back_split[:, 1:],
        preferred_element_type=jnp.float32,
    )
    grad_input_norm, grad_gain_first, grad_bias_first = norm_first_back(grad_normed_attn)
    grad_images = (grad_residual + grad_input_norm).astype(jnp.bfloat16)
    (
        part_gone,
        part_bone,
        part_qkv,
        part_qvb,
        part_outw,
        part_outb,
        part_gtwo,
        part_btwo,
        part_up,
        part_upb,
        part_down,
        part_downb,
    ) = (
        lax.psum_scatter(
            grad_gain_first.astype(jnp.bfloat16), "fsdp", scatter_dimension=0, tiled=True
        ).astype(jnp.float32),
        lax.psum_scatter(
            grad_bias_first.astype(jnp.bfloat16), "fsdp", scatter_dimension=0, tiled=True
        ).astype(jnp.float32),
        lax.psum_scatter(
            grad_qkv.astype(jnp.bfloat16), "fsdp", scatter_dimension=0, tiled=True
        ).astype(jnp.float32),
        lax.psum_scatter(
            grad_qvb.astype(jnp.bfloat16), "fsdp", scatter_dimension=1, tiled=True
        ).astype(jnp.float32),
        lax.psum_scatter(
            grad_outw.astype(jnp.bfloat16), "fsdp", scatter_dimension=0, tiled=True
        ).astype(jnp.float32),
        lax.psum_scatter(
            grad_outb.astype(jnp.bfloat16), "fsdp", scatter_dimension=0, tiled=True
        ).astype(jnp.float32),
        lax.psum_scatter(
            grad_gain_second.astype(jnp.bfloat16), "fsdp", scatter_dimension=0, tiled=True
        ).astype(jnp.float32),
        lax.psum_scatter(
            grad_bias_second.astype(jnp.bfloat16), "fsdp", scatter_dimension=0, tiled=True
        ).astype(jnp.float32),
        lax.psum_scatter(
            grad_up.astype(jnp.bfloat16), "fsdp", scatter_dimension=0, tiled=True
        ).astype(jnp.float32),
        lax.psum_scatter(
            grad_upb.astype(jnp.bfloat16), "fsdp", scatter_dimension=0, tiled=True
        ).astype(jnp.float32),
        lax.psum_scatter(
            grad_down.astype(jnp.bfloat16), "fsdp", scatter_dimension=1, tiled=True
        ).astype(jnp.float32),
        lax.psum_scatter(
            grad_downb.astype(jnp.bfloat16), "fsdp", scatter_dimension=0, tiled=True
        ).astype(jnp.float32),
    )
    (
        final_gone,
        final_bone,
        final_qkv,
        final_qvb,
        final_outw,
        final_outb,
        final_gtwo,
        final_btwo,
        final_up,
        final_upb,
        final_down,
        final_downb,
    ) = (
        lax.psum(part_gone.astype(jnp.bfloat16), "seq").astype(jnp.float32),
        lax.psum(part_bone.astype(jnp.bfloat16), "seq").astype(jnp.float32),
        lax.psum(part_qkv.astype(jnp.bfloat16), "seq").astype(jnp.float32),
        lax.psum(part_qvb.astype(jnp.bfloat16), "seq").astype(jnp.float32),
        lax.psum(part_outw.astype(jnp.bfloat16), "seq").astype(jnp.float32),
        lax.psum(part_outb.astype(jnp.bfloat16), "seq").astype(jnp.float32),
        lax.psum(part_gtwo.astype(jnp.bfloat16), "seq").astype(jnp.float32),
        lax.psum(part_btwo.astype(jnp.bfloat16), "seq").astype(jnp.float32),
        lax.psum(part_up.astype(jnp.bfloat16), "seq").astype(jnp.float32),
        lax.psum(part_upb.astype(jnp.bfloat16), "seq").astype(jnp.float32),
        lax.psum(part_down.astype(jnp.bfloat16), "seq").astype(jnp.float32),
        lax.psum(part_downb.astype(jnp.bfloat16), "seq").astype(jnp.float32),
    )
    return (
        layer_out,
        grad_images,
        final_gone,
        final_bone,
        final_qkv,
        final_qvb,
        final_outw,
        final_outb,
        final_gtwo,
        final_btwo,
        final_up,
        final_upb,
        final_down,
        final_downb,
    )


def solution(mesh):
    placed = (
        P("fsdp", "seq", None),
        P("fsdp"),
        P("fsdp"),
        P("fsdp"),
        P("fsdp", None),
        P(None, "fsdp"),
        P("fsdp", None),
        P("fsdp"),
        P("fsdp"),
        P("fsdp"),
        P("fsdp", None),
        P("fsdp"),
        P(None, "fsdp"),
        P("fsdp"),
        P("fsdp", "seq", None),
    )
    return jax.shard_map(
        on_device,
        mesh=mesh,
        in_specs=placed,
        out_specs=(
            P("fsdp", "seq", None),
            P("fsdp", "seq", None),
            P("fsdp"),
            P("fsdp"),
            P("fsdp", None),
            P(None, "fsdp"),
            P("fsdp", None),
            P("fsdp"),
            P("fsdp"),
            P("fsdp"),
            P("fsdp", None),
            P("fsdp"),
            P(None, "fsdp"),
            P("fsdp"),
        ),
        check_vma=False,
    )
```

profile of v0, /device:TPU:0, one launch (start us, length us, event | category | flops | bytes accessed | tf_op | source)
XLA Modules:
  0.0 1667.9 jit_solution(1936642603031009704)
XLA Ops:
  13.0 18.5 %all-reduce.17 = (bf16[1152]{0:T(1024)(128)(2,1)S(1)}, bf16[1152]{0:T(1024)(128)(2,1)S(1)}, bf16[1152]{0:T(1024)(128)(2,1)S(1)}, bf16[1152]{0:T(1024)(128)(2,1)S...) all-reduce(bf16[1152]{0:T(1024)(128)(2,1)S(1)} %dynamic-update-slic, ...), channel_id=1, replica_groups=mesh['fsdp'=4,'seq'=8] {'fsdp'}, use_global_device_ids=true, to_apply=%add.1 | all-reduce | flops 10064 | bytes 40256
  33.3 7.5 all-gather
  41.1 55.8 %all-gather.6.cloned.1.call-done = bf16[1152,3456]{1,0:T(8,128)(2,1)} async-done(((bf16[288,3456]{1,0:T(8,128)(2,1)}), bf16[1152,3456]{1,0:T(8,128)(2,1)}) %all-gather.6.cloned.1.call-update) | async-done | bytes 7962640 | tf_op jit(solution)/shard_map/all_gather | solution.py:115
  96.9 11.5 copy.97
  108.5 12.5 convolution_bitcast_fusion.3
  133.9 155.1 %all-to-all-done = bf16[3,16,8,72,128]{4,3,0,2,1:T(8,128)(2,1)} async-done(((bf16[3,16,8,72,128]{4,3,0,2,1:T(8,128)(2,1)}), bf16[3,16,8,72,128]{4,3,0,2,1:T(8,128)(2,1)}, u32[]{:S(2)}, u32[]{:S(2)}) %all-to-all-start) | async-done | bytes 7077920 | tf_op jit(solution)/shard_map/all_to_all | solution.py:133
  289.0 7.7 fusion.114
  325.3 180.0 %while.26 = (s32[]{:T(128)}, bf16[16,72,1024]{2,1,0:T(8,128)(2,1)}, f32[16,1024]{1,0:T(8,128)}, bf16[16,72,1024]{2,1,0:T(8,128)(2,1)}, s32[16]{0:T(128)S(1)}, /*...) while((s32[]{:T(128)}, bf16[16,72,1024]{2,1,0:T(8,128)(2,1)}, ...), condition=%wide.region_5.6_spmd, body=%wide.region_2.5_spmd.sunk | while | flops 311500800 | bytes 29997196 | solution.py:140
  505.4 6.3 copy.103
  516.7 93.5 %all-to-all-done.1 = bf16[2,8,72,1024]{2,1,0,3:T(8,128)(2,1)} async-done(((bf16[2,8,72,1024]{2,1,0,3:T(8,128)(2,1)}), bf16[2,8,72,1024]{2,1,0,3:T(8,128)(2,1)}, u32[]{:S(2)}, u32[]{:S(2)}) %all-to-all-start.1) | async-done | bytes 2359328 | tf_op jit(solution)/shard_map/all_to_all | solution.py:143
  616.5 6.5 fusion.116
  625.9 24.8 %multiply_convert_fusion.1 = (bf16[8,128,4304]{1,2,0:T(8,128)(2,1)}, f32[8,128,4304]{1,2,0:T(8,128)}) fusion(f32[4304]{0:T(1024)S(1)} %convert_element_type.186, bf16[1152,4304]{1,0:T(8,128)(2,1)} %all-gather.10.cloned.1.call-done, f32[8,128,1152]{2,1,0:T(8,128)} %copy-done.5, f32[1152]{0:T(1024)S(1)} %convert_element_type.184, ...), kind=kOutput, calls=%fused_computation.72 | convolution fusion | flops 10204381184 | bytes 41113408 | tf_op jit(solution)/shard_map/itd,df->itf/dot_general | solution.py:168
  650.7 32.5 %fusion.117 = (bf16[4304]{0:T(1024)(128)(2,1)}, bf16[8,128,4304]{1,2,0:T(8,128)(2,1)}) fusion(f32[8,128,4304]{1,2,0:T(8,128)} %get-tuple-element.199, f32[4304]{0:T(1024)S(1)} %convert_element_type.186, bf16[8,128,1152]{2,1,0:T(8,128)(2,1)} %param.34, bf16[4304,1152]{0,1:T(8,128)(2,1)} %all-gather.12.cloned.1.call-done), kind=kOutput, calls=%fused_computation.155 | convolution fusion | flops 10251366400 | bytes 38745312 | tf_op jit(solution)/shard_map/itd,fd->itf/dot_general | solution.py:189
  683.2 20.6 %multiply_reduce_fusion.1 = (bf16[1152]{0:T(1024)(128)(2,1)}, f32[8,128]{1,0:T(8,128)S(1)}, bf16[1152]{0:T(1024)(128)(2,1)}, f32[8,128,1152]{2,1,0:T(8,128)}) fusion(f32[8,128,1152]{2,1,0:T(8,128)S(1)} %bitcast.254, f32[8,128]{1,0:T(8,128)S(1)} %fusion.109, f32[8,128]{1,0:T(8,128)S(1)} %broadcast_multiply_fusion, f32[1152]{0:T(1024)S(1)} %convert_element_type.183, ...), kind=kOutput, calls=%fused_computation.117 | convolution fusion | flops 10163844096 | bytes 28189696 | tf_op jit(solution)/shard_map/itf,df->itd/dot_general | solution.py:194
  715.4 19.1 %fusion.54 = bf16[1152,4304]{1,0:T(8,128)(2,1)} fusion(bf16[8,128,4304]{1,2,0:T(8,128)(2,1)} %get-tuple-element.203, f32[8,128,1152]{2,1,0:T(8,128)} %copy-done.5, f32[1152]{0:T(1024)S(1)} %convert_element_type.184, f32[1152]{0:T(1024)S(1)} %convert_element_type.183, f32[8,128]{1,0:T(8,128)S(1)} %fusion.109, f32[8,128]{1,0:T(8,128)S(1)} %broadcast_multiply_fusion), kind=kOutput, calls=%fused_computation.63 | convolution fusion | flops 10165266432 | bytes 23467008 | tf_op jit(solution)/shard_map/itd,itf->df/dot_general | solution.py:192
  747.3 16.5 fusion.55
  764.1 37.8 %all-to-all-done.2 = bf16[16,8,72,128]{3,2,1,0:T(8,128)(2,1)} async-done(((bf16[16,8,72,128]{3,2,1,0:T(8,128)(2,1)}), bf16[16,8,72,128]{3,2,1,0:T(8,128)(2,1)}, u32[]{:S(2)}, u32[]{:S(2)}) %all-to-all-start.2) | async-done | bytes 2359328 | tf_op jit(solution)/shard_map/all_to_all | solution.py:208
  811.2 220.9 %while.27 = (s32[]{:T(128)}, bf16[16,72,1024]{2,1,0:T(8,128)(2,1)S(1)}, bf16[16,72,1024]{2,1,0:T(8,128)(2,1)}, bf16[16,72,1024]{2,1,0:T(8,128)(2,1)}, bf16[16,72...) while((s32[]{:T(128)}, ...), condition=%wide.region_12.13_spmd, body=%wide.region_10.12_spmd.sunk | while | flops 767778816 | bytes 32969856 | solution.py:210
  1037.0 6.4 copy.109
  1049.7 6.9 pad_maximum_fusion
  1056.7 277.4 %all_to_all.66 = bf16[3,2,8,72,1024]{3,2,1,0,4:T(8,128)(2,1)} all-to-all(bf16[3,2,8,72,1024]{3,2,1,0,4:T(8,128)(2,1)S(1)} %pad_maximum_fusion), channel_id=1, replica_groups=mesh['fsdp'=4,'seq'=8] {'seq'}, dimensions={4} | all-to-all | bytes 14155776 | tf_op jit(solution)/shard_map/all_to_all | solution.py:215
  1334.1 15.4 copy.114
  1349.5 13.9 fusion.63
  1363.4 11.6 copy.115
  1376.8 13.2 copy.133
  1411.4 8.9 fusion.110
  1424.5 17.1 %all-reduce.16 = (bf16[1152]{0:T(1024)(128)(2,1)S(1)}, bf16[1152]{0:T(1024)(128)(2,1)S(1)}, bf16[1152]{0:T(1024)(128)(2,1)S(1)}, bf16[1152]{0:T(1024)(128)(2,1)S...) all-reduce(bf16[1152]{0:T(1024)(128)(2,1)S(1)} %dynamic-update-slic, ...), channel_id=1, replica_groups=mesh['fsdp'=4,'seq'=8] {'fsdp'}, use_global_device_ids=true, to_apply=%add.6 | all-reduce | flops 12368 | bytes 49472
  1442.2 15.3 reduce-scatter.8.cloned.1.call-done
  1457.5 6.5 add_convert_fusion
  1464.1 19.0 %fusion.94 = bf16[8,128,1152]{2,1,0:T(8,128)(2,1)} fusion(f32[8,128,1152]{2,1,0:T(8,128)} %copy-done.5, bf16[8,128,4304]{1,2,0:T(8,128)(2,1)} %get-tuple-element.198, bf16[4304,1152]{0,1:T(8,128)(2,1)} %all-gather.12.cloned.1.call-done, f32[1152]{0:T(1024)S(1)} %convert_element_type.188), kind=kOutput, calls=%fused_computation.123 | convolution fusion | flops 10157948928 | bytes 25813504 | tf_op jit(solution)/shard_map/itf,fd->itd/dot_general | solution.py:175
  1486.2 29.3 %all-reduce.14 = (bf16[288]{0:T(512)(128)(2,1)S(1)}, bf16[288]{0:T(512)(128)(2,1)S(1)}, bf16[2,288]{1,0:T(2,128)(2,1)S(1)}, bf16[288]{0:T(512)(128)(2,1)S(1)}, b...) all-reduce(bf16[288]{0:T(512)(128)(2,1)S(1)} %dynamic-slice.8, ...), channel_id=1, replica_groups=mesh['fsdp'=4,'seq'=8] {'seq'}, use_global_device_ids=true, to_apply=%region_17.18 | all-reduce | flops 3380 | bytes 13520 | tf_op jit(solution)/shard_map/psum | solution.py:304
  1520.2 130.0 %all-reduce.20.cloned.1.call-done = (bf16[288,3456]{1,0:T(8,128)(2,1)}, bf16[288,1152]{1,0:T(8,128)(2,1)}, bf16[288,4304]{1,0:T(8,128)(2,1)}, bf16[4304,288]{0,1:T(8,128)(2,1)}) async-done(((bf16[288,3456]{1,0:T(8,128)(2,1)}, bf16[288,1152]{1,0:T(8,128)(2,1)}, bf16[288,4304]{1,0:T(8,128)(2,1)}, bf16[4304,288]{0,1:T(8,128)(2,1)}), (bf16[288,3456]{1,0:T(8,128)(2,1)}, bf16[288,1152]{1,0:T(8,128)(2,1)}, ...) | async-done | bytes 7612432 | tf_op jit(solution)/shard_map/psum | solution.py:306
  (518 shorter events, 551.6 us)
Async XLA Ops:
  7.3 24.2 %copy-start.2 = (bf16[8,128,1152]{2,1,0:T(8,128)(2,1)S(1)}, bf16[8,128,1152]{2,1,0:T(8,128)(2,1)}, u32[]{:S(2)}) copy-start(bf16[8,128,1152]{2,1,0:T(8,128)(2,1)} %param.20) | copy-start | bytes 7077892
  7.3 26.0 %copy-start.34 = (bf16[2,288]{1,0:T(2,128)(2,1)S(1)}, bf16[2,288]{1,0:T(2,128)(2,1)}, u32[]{:S(2)}) copy-start(bf16[2,288]{1,0:T(2,128)(2,1)} %param.25) | copy-start | bytes 3460
  7.3 89.6 %all-gather.6.cloned.1.call-start = ((), (), s32[]{:S(2)}) async-start(), calls=%async_computation.9 | async-start | bytes 9953280 | tf_op jit(solution)/shard_map/all_gather | solution.py:115
  8.0 608.5 %all-gather.8.cloned.1.call-start = ((), (), s32[]{:S(2)}) async-start(), calls=%async_computation.10 | async-start | bytes 3317760 | tf_op jit(solution)/shard_map/all_gather | solution.py:117
  8.8 617.1 %all-gather.10.cloned.1.call-start = ((), (), s32[]{:S(2)}) async-start(), calls=%async_computation.11 | async-start | bytes 12533760 | tf_op jit(solution)/shard_map/all_gather | solution.py:159
  31.5 77.0 %copy-start.15 = (f32[1152]{0:T(1024)}, f32[1152]{0:T(1024)S(1)}, u32[]{:S(2)}) copy-start(f32[1152]{0:T(1024)S(1)} %convert_element_type.178) | copy-start | bytes 13828
  31.5 77.0 %copy-start.28 = (f32[1152]{0:T(1024)}, f32[1152]{0:T(1024)S(1)}, u32[]{:S(2)}) copy-start(f32[1152]{0:T(1024)S(1)} %convert_element_type.179) | copy-start | bytes 13828
  31.9 76.6 %copy-start.17 = (f32[8,128]{1,0:T(8,128)}, f32[8,128]{1,0:T(8,128)S(1)}, u32[]{:S(2)}) copy-start(f32[8,128]{1,0:T(8,128)S(1)} %broadcast_multiply_fusion.1) | copy-start | bytes 12292
  32.7 75.8 %copy-start.21 = (f32[8,128]{1,0:T(8,128)}, f32[8,128]{1,0:T(8,128)S(1)}, u32[]{:S(2)}) copy-start(f32[8,128]{1,0:T(8,128)S(1)} %fusion.108) | copy-start | bytes 12292
  128.3 160.7 %all-to-all-start = ((bf16[3,16,8,72,128]{4,3,0,2,1:T(8,128)(2,1)}), bf16[3,16,8,72,128]{4,3,0,2,1:T(8,128)(2,1)}, u32[]{:S(2)}, u32[]{:S(2)}) async-start(bf16[3,16,8,72,128]{4,3,0,2,1:T(8,128)(2,1)} %copy.99), calls=%async_computation | async-start | bytes 14155776 | tf_op jit(solution)/shard_map/all_to_all | solution.py:133
  133.2 517.4 %all-gather.12.cloned.1.call-start = ((), (), s32[]{:S(2)}) async-start(), calls=%async_computation.12 | async-start | bytes 12533760 | tf_op jit(solution)/shard_map/all_gather | solution.py:161
  505.4 6.3 copy-start.42
  511.7 98.5 %all-to-all-start.1 = ((bf16[2,8,72,1024]{2,1,0,3:T(8,128)(2,1)}), bf16[2,8,72,1024]{2,1,0,3:T(8,128)(2,1)}, u32[]{:S(2)}, u32[]{:S(2)}) async-start(bf16[2,8,72,1024]{2,1,0,3:T(8,128)(2,1)} %bitcast.255), calls=%async_computation.1 | async-start | bytes 8388608 | tf_op jit(solution)/shard_map/all_to_all | solution.py:143
  516.2 926.0 %reduce-scatter.10.cloned.1.call-start = ((), (), s32[]{:S(2)}) async-start(), calls=%async_computation.14 | async-start | bytes 3317760 | tf_op jit(solution)/shard_map/reduce_scatter | solution.py:265
  625.9 57.3 %slice-start = ((s8[4718592]{0:T(1024)(128)(4,1)}), s8[524288]{0:T(1024)(128)(4,1)S(1)}, s32[]{:S(2)}) async-start(s8[4718592]{0:T(1024)(128)(4,1)} %bitcast.253), calls=%async_computation.19 | async-start | bytes 1048576
  650.7 32.5 %slice-start.1 = ((s8[4718592]{0:T(1024)(128)(4,1)}), s8[4194304]{0:T(1024)(128)(4,1)S(1)}, s32[]{:S(2)}) async-start(s8[4718592]{0:T(1024)(128)(4,1)} %bitcast.253), calls=%async_computation.20 | async-start | bytes 8388608
  715.4 726.9 %reduce-scatter.12.cloned.1.call-start = ((), (), s32[]{:S(2)}) async-start(), calls=%async_computation.15 | async-start | bytes 12533760 | tf_op jit(solution)/shard_map/reduce_scatter | solution.py:277
  741.1 6.2 copy-start.8
  742.9 59.0 %all-to-all-start.2 = ((bf16[16,8,72,128]{3,2,1,0:T(8,128)(2,1)}), bf16[16,8,72,128]{3,2,1,0:T(8,128)(2,1)}, u32[]{:S(2)}, u32[]{:S(2)}) async-start(bf16[16,8,72,128]{3,2,1,0:T(8,128)(2,1)} %copy.106), calls=%async_computation.2 | async-start | bytes 4718592 | tf_op jit(solution)/shard_map/all_to_all | solution.py:208
  747.2 695.0 %reduce-scatter.14.cloned.1.call-start = ((), (), s32[]{:S(2)}) async-start(), calls=%async_computation.16 | async-start | bytes 12533760 | tf_op jit(solution)/shard_map/reduce_scatter | solution.py:283
  763.8 693.7 %reduce-scatter.8.cloned.1.call-start = ((), (), s32[]{:S(2)}) async-start(), calls=%async_computation.13 | async-start | bytes 9953280 | tf_op jit(solution)/shard_map/reduce_scatter | solution.py:259
  1334.0 15.4 copy-start.3
  1334.0 15.4 copy-start.16
  1334.0 15.4 copy-start.18
  1334.0 15.4 copy-start.22
  1334.0 15.4 copy-start.29
  1334.1 15.4 copy-start.44
  1375.0 110.2 %reduce-scatter.16.cloned.1.call-start = ((), (), s32[]{:S(2)}) async-start(), calls=%async_computation.17 | async-start | bytes 368640
  1404.5 6.8 slice-start.2
  1411.4 8.9 copy-start.24
  1420.4 229.8 %all-reduce.20.cloned.1.call-start = ((), (), s32[]{:S(2)}) async-start(), calls=%async_computation.18 | async-start | bytes 15335424 | tf_op jit(solution)/shard_map/psum | solution.py:306
  1424.4 33.1 %copy-start.20 = (f32[8,128]{1,0:T(8,128)S(1)}, f32[8,128]{1,0:T(8,128)}, u32[]{:S(2)}) copy-start(f32[8,128]{1,0:T(8,128)} %copy-done.19) | copy-start | bytes 12292
  (45 other events, 137.1 us)
Sparse Core Ops, SparseCore 0:
  9.9 86.9 all-gather.5
  98.8 39.7 all-gather.7
  140.4 101.0 all-gather.9
  243.3 101.0 all-gather.11
  715.5 38.3 reduce-scatter.9
  756.9 99.6 reduce-scatter.11
  859.8 99.6 reduce-scatter.13
  1375.1 82.3 reduce-scatter.7
  1460.8 24.3 reduce-scatter.15
  1487.7 162.3 all-reduce.19
where the time goes:
time: 1680 us; the launch traced here: 1670 us
  waiting for transfers between devices  492 us (29%)
  matrix products  447 us (27%)
  blocking collectives  350 us (21%)
  local copies, waits for them, and re-layouts  242 us (14%)
  other arithmetic  102 us (6%)
  between operations  18 us (1%)
    all_to_all x1, blocking collectives, on_device(): lax.all_to_all(for_sending(grad_stack), 'seq', split_axis=4, concat_axis=...  277 us
    all_to_all x1, waiting for transfers between devices, on_device(): lax.all_to_all(stacked, 'seq', split_axis=1, concat_axis=4, tiled=True)  155 us
    psum x1, waiting for transfers between devices, on_device(): lax.psum(part_qkv.astype(jnp.bfloat16), 'seq').astype(jnp.float32)  130 us
    all_to_all x1, waiting for transfers between devices, on_device(): lax.all_to_all(for_sending(mixed_items.reshape(local_heads, image_count,...  93.5 us
    dot_general x16, matrix products, attend_item(): jnp.einsum('qk,dk->dq', softmax_low, values, preferred_element_type=jnp.f...  64.5 us
    all_gather x1, waiting for transfers between devices, on_device(): lax.all_gather(w_qkv, 'fsdp', axis=0, tiled=True)  55.8 us
    dot_general x16, matrix products, attend_back(): jnp.einsum('qk,dq->dk', softmax_out.astype(jnp.bfloat16), grad_rows, pref...  42.4 us
    all_to_all x1, waiting for transfers between devices, on_device(): lax.all_to_all(grad_mixed, 'seq', split_axis=0, concat_axis=3, tiled=True)  37.8 us
  transfers between devices with their start and end apart: 13, of which 7 were waited for; matrix products, arithmetic and copies ran while one was open for 41% of the time, Pallas kernels for 0%

commit v1 on v0

v1 whole, which is shorter than its diff:
```python
import functools
import math

import jax
import jax.numpy as jnp
from jax import lax
from jax.experimental import pallas as pl
from jax.experimental.pallas import tpu as pltpu
from jax.sharding import Mesh
from jax.sharding import PartitionSpec as P

H = 16
HD = 72
WIDTH = H * HD
EPS = 1e-06
LOG2E = math.log2(math.e)
BF = jnp.bfloat16
F32 = jnp.float32
SEQ = ("z", "core")


def nt(a, b):
    return lax.dot_general(a, b, (((1,), (1,)), ((), ())), preferred_element_type=F32)


def nn(a, b):
    return lax.dot_general(a, b, (((1,), (0,)), ((), ())), preferred_element_type=F32)


def tn(a, b):
    return lax.dot_general(a, b, (((0,), (0,)), ((), ())), preferred_element_type=F32)


def head_window(h):
    start = jnp.minimum((h * HD) // 128 * 128, WIDTH - 256)
    offset = h * HD - start
    lane = lax.broadcasted_iota(jnp.int32, (1, 256), 1)
    return pl.multiple_of(start, 128), (lane >= offset) & (lane < offset + HD)


def forward_kernel(block, q_ref, k_ref, v_ref, bias_ref, out_ref, lse_ref, total, stats):
    h = pl.program_id(0)

    @pl.when(h == 0)
    def _():
        total[...] = jnp.zeros_like(total)
        stats[...] = jnp.zeros_like(stats)

    start, mask = head_window(h)
    window = pl.ds(start, 256)
    k = k_ref[:, window]
    v = v_ref[:, window]
    bias = bias_ref[...]
    mine = lax.broadcasted_iota(jnp.int32, (1, 128), 1) == h
    for b in range(q_ref.shape[0] // block):
        rows = pl.ds(b * block, block)
        q = jnp.where(mask, q_ref[rows, window], 0)
        scores = nt(q, k) + bias
        top = jnp.max(scores, -1, keepdims=True)
        weights = jnp.exp2(scores - top)
        norm = jnp.sum(weights, -1, keepdims=True)
        mixed = nn(weights.astype(BF), v)
        total[rows, window] += jnp.where(mask, mixed * (1.0 / norm), 0.0)
        stats[rows, :] += jnp.where(mine, top + jnp.log2(norm), 0.0)

    @pl.when(h == H - 1)
    def _():
        out_ref[...] = total[...].astype(out_ref.dtype)
        lse_ref[...] = stats[...].T[:H]


def column_block(rows, index):
    return pl.BlockSpec((rows, WIDTH), lambda h: (0, index))


def whole(shape):
    return pl.BlockSpec(shape, lambda h: (0,) * len(shape))


def attend(qkv, keys, values, places, bias):
    tokens, key_count = qkv.shape[0], keys.shape[0]
    return pl.pallas_call(
        functools.partial(forward_kernel, 256),
        grid=(H,),
        in_specs=[
            column_block(tokens, 0),
            column_block(key_count, places[0]),
            column_block(key_count, places[1]),
            whole((1, key_count)),
        ],
        out_specs=[whole((tokens, WIDTH)), whole((H, tokens))],
        out_shape=[
            jax.ShapeDtypeStruct((tokens, WIDTH), BF),
            jax.ShapeDtypeStruct((H, tokens), F32),
        ],
        scratch_shapes=[pltpu.VMEM((tokens, WIDTH), F32), pltpu.VMEM((tokens, 128), F32)],
        compiler_params=pltpu.CompilerParams(
            dimension_semantics=("arbitrary",), vmem_limit_bytes=60 << 20
        ),
        cost_estimate=pl.CostEstimate(
            flops=4 * H * tokens * key_count * 256,
            bytes_accessed=8 * tokens * WIDTH,
            transcendentals=H * tokens * key_count,
        ),
        name="attend",
    )(qkv, keys, values, bias)


def backward_kernel(
    block,
    q_ref,
    k_ref,
    v_ref,
    grad_ref,
    lse_ref,
    delta_ref,
    bias_ref,
    dq_ref,
    dk_ref,
    dv_ref,
    dq_sum,
    dk_sum,
    dv_sum,
):
    h = pl.program_id(0)

    @pl.when(h == 0)
    def _():
        dq_sum[...] = jnp.zeros_like(dq_sum)
        dk_sum[...] = jnp.zeros_like(dk_sum)
        dv_sum[...] = jnp.zeros_like(dv_sum)

    start, mask = head_window(h)
    window = pl.ds(start, 256)
    q = jnp.where(mask, q_ref[:, window], 0)
    grad = jnp.where(mask, grad_ref[:, window], 0)
    lse = lse_ref[pl.ds(h, 1), :]
    delta = delta_ref[pl.ds(h, 1), :]
    dq = None
    for b in range(k_ref.shape[0] // block):
        rows = pl.ds(b * block, block)
        k = jnp.where(mask, k_ref[rows, window], 0)
        v = v_ref[rows, window]
        weights = jnp.exp2(nt(k, q) + bias_ref[rows, :] - lse)
        dscores = (weights * (nt(v, grad) - delta)).astype(BF)
        dv_sum[rows, window] += nn(weights.astype(BF), grad)
        dk_sum[rows, window] += nn(dscores, q)
        part = nn(k.T, dscores)
        dq = part if dq is None else dq + part
    dq_sum[:, window] += dq.T

    @pl.when(h == H - 1)
    def _():
        dq_ref[...] = (dq_sum[...] * HD**-0.5).astype(dq_ref.dtype)
        dk_ref[...] = (dk_sum[...] * (1.0 / LOG2E)).astype(dk_ref.dtype)
        dv_ref[...] = dv_sum[...].astype(dv_ref.dtype)


def joined_kernel(*refs):
    *inputs, out_ref, dq_sum, dk_sum, dv_sum = refs
    views = [out_ref.at[:, pl.ds(i * WIDTH, WIDTH)] for i in range(3)]
    backward_kernel(256, *inputs, *views, dq_sum, dk_sum, dv_sum)


def attend_back(qkv, keys, values, places, grad, lse, delta, bias):
    tokens, key_count = qkv.shape[0], keys.shape[0]
    joined = tokens == key_count
    if joined:
        body = joined_kernel
        shapes = [(tokens, 3 * WIDTH)]
    else:
        body = functools.partial(backward_kernel, 256)
        shapes = [(tokens, WIDTH), (key_count, WIDTH), (key_count, WIDTH)]
    return pl.pallas_call(
        body,
        grid=(H,),
        in_specs=[
            column_block(tokens, 0),
            column_block(key_count, places[0]),
            column_block(key_count, places[1]),
            whole((tokens, WIDTH)),
            whole((H, tokens)),
            whole((H, tokens)),
            whole((key_count, 1)),
        ],
        out_specs=[whole(s) for s in shapes],
        out_shape=[jax.ShapeDtypeStruct(s, BF) for s in shapes],
        scratch_shapes=[
            pltpu.VMEM((tokens, WIDTH), F32),
            pltpu.VMEM((key_count, WIDTH), F32),
            pltpu.VMEM((key_count, WIDTH), F32),
        ],
        compiler_params=pltpu.CompilerParams(
            dimension_semantics=("arbitrary",), vmem_limit_bytes=62 << 20
        ),
        cost_estimate=pl.CostEstimate(
            flops=10 * H * tokens * key_count * 256,
            bytes_accessed=14 * tokens * WIDTH,
            transcendentals=H * tokens * key_count,
        ),
        name="attend_back",
    )(qkv, keys, values, grad, lse, delta, bias)


def normal(field):
    mean = jnp.mean(field, -1, keepdims=True)
    centered = field - mean
    rate = lax.rsqrt(jnp.mean(centered * centered, -1, keepdims=True) + EPS)
    return centered * rate, rate


def normal_back(upstream, gain, unit, rate):
    scaled = upstream * gain
    mean = jnp.mean(scaled, -1, keepdims=True)
    along = jnp.mean(scaled * unit, -1, keepdims=True)
    return rate * (scaled - mean - unit * along)


def flip(array, bit):
    return lax.ppermute(array, "fsdp", [(i, i ^ bit) for i in range(4)])


def swap_core(array):
    return lax.ppermute(array, "core", [(0, 1), (1, 0)])


def gather_rows(shard, parts):
    rows, columns = shard.shape
    if parts != 4:
        return lax.all_gather(shard, "fsdp", axis=0, tiled=True)
    me, core = lax.axis_index("fsdp"), lax.axis_index("core")
    half = rows // 2
    own = lax.dynamic_slice_in_dim(shard, core * half, half, 0)
    near_x, near_y = flip(own, 1), flip(own, 2)
    quarter = half // 2
    far_a = flip(near_x[:quarter], 2)
    far_b = flip(near_y[quarter:], 1)
    held = jnp.zeros((4, half, columns), shard.dtype)
    held = lax.dynamic_update_slice(held, own[None], (me, 0, 0))
    held = lax.dynamic_update_slice(held, near_x[None], (me ^ 1, 0, 0))
    held = lax.dynamic_update_slice(held, near_y[None], (me ^ 2, 0, 0))
    held = lax.dynamic_update_slice(held, far_a[None], (me ^ 3, 0, 0))
    held = lax.dynamic_update_slice(held, far_b[None], (me ^ 3, quarter, 0))
    other = swap_core(held)
    first = jnp.where(core == 0, held, other)
    second = jnp.where(core == 0, other, held)
    return jnp.stack([first, second], 1).reshape(4 * rows, columns)


def reduce_rows(grad, parts):
    rows, columns = grad.shape[0] // parts, grad.shape[1]
    core = lax.axis_index("core")
    half = rows // 2
    split = grad.astype(BF).reshape(parts, 2, half, columns)
    keep = lax.dynamic_index_in_dim(split, core, 1, keepdims=False)
    give = lax.dynamic_index_in_dim(split, 1 - core, 1, keepdims=False)
    pair = (keep.astype(F32) + swap_core(give).astype(F32)).astype(BF)
    spread = lax.all_to_all(pair, "fsdp", 0, 0, tiled=True)
    local = jnp.sum(spread.astype(F32), 0).astype(BF)
    local = lax.psum(local, "z")
    other = swap_core(local)
    first = jnp.where(core == 0, local, other)
    second = jnp.where(core == 0, other, local)
    return jnp.concatenate([first, second], 0).astype(F32)


def on_device(
    images,
    lengths,
    ln1_gain,
    ln1_bias,
    w_qkv,
    qv_bias,
    w_out,
    out_bias,
    ln2_gain,
    ln2_bias,
    w_up,
    up_bias,
    w_down,
    down_bias,
    cotangent,
):
    group, local_tokens, width = images.shape
    parts = lax.axis_size("fsdp")
    seq = lax.axis_size(SEQ)
    share = seq // group
    piece = local_tokens // share
    tokens = seq * piece
    key_count = tokens * share
    scale = HD**-0.5

    def to_image(field):
        moved = lax.all_to_all(field.reshape(seq, piece, width), SEQ, 0, 0, tiled=True)
        return moved.reshape(tokens, width)

    def to_tokens(field):
        moved = lax.all_to_all(field.reshape(seq, piece, width), SEQ, 0, 0, tiled=True)
        return moved.reshape(group, local_tokens, width)

    x_low = to_image(images)
    cot_low = to_image(cotangent)

    vectors = [ln1_gain, ln1_bias, qv_bias[0], qv_bias[1], out_bias, ln2_gain, ln2_bias, down_bias, up_bias]
    sizes = [v.shape[0] for v in vectors]
    packed = lax.all_gather(jnp.concatenate(vectors), "fsdp", axis=0)
    full, at = [], 0
    for size in sizes:
        full.append(packed[:, at : at + size].reshape(1, parts * size).astype(F32))
        at += size
    gain1, shift1, q_bias, v_bias, o_bias, gain2, shift2, d_bias, u_bias = full

    qkv_w = gather_rows(w_qkv, parts)
    out_w = gather_rows(w_out, parts)
    up_w = gather_rows(w_up, parts)
    down_w = gather_rows(w_down.T, parts)

    row = jnp.arange(key_count)
    place = (row % tokens) // piece * local_tokens + row // tokens * piece + row % piece
    image = lax.axis_index(SEQ) // share
    length = lax.dynamic_index_in_dim(lengths, image, 0, keepdims=False)
    bias = jnp.where(place < length, 0.0, -1e30).astype(F32)

    x = x_low.astype(F32)
    unit1, rate1 = normal(x)
    normed1 = (unit1 * gain1 + shift1).astype(BF)
    column_bias = jnp.concatenate([q_bias, jnp.zeros_like(q_bias), v_bias], 1)
    column_scale = jnp.where(jnp.arange(3 * width) < width, scale * LOG2E, 1.0)[None]
    qkv = ((nn(normed1, qkv_w) + column_bias) * column_scale).astype(BF)
    if share == 1:
        keys, values, places = qkv, qkv, (1, 2)
    else:
        both = lax.all_gather(qkv[:, width:], "core", axis=0, tiled=True)
        keys, values, places = both, both, (0, 1)
    attended, lse = attend(qkv, keys, values, places, bias[None])
    residual = x + nn(attended, out_w) + o_bias
    unit2, rate2 = normal(residual)
    normed2 = (unit2 * gain2 + shift2).astype(BF)
    pre = nn(normed2, up_w) + u_bias
    inner = math.sqrt(2 / math.pi)
    tanh = jnp.tanh(inner * (pre + 0.044715 * pre * pre * pre))
    activation = (0.5 * pre * (1 + tanh)).astype(BF)
    slope = 0.5 * (1 + tanh) + 0.5 * pre * (1 - tanh * tanh) * inner * (1 + 3 * 0.044715 * pre * pre)
    slope = slope.astype(BF)
    layer_out = (residual + nt(activation, down_w) + d_bias).astype(BF)
    layer_out = to_tokens(layer_out)

    grad_pre = (nn(cot_low, down_w) * slope).astype(BF)
    grad_down = reduce_rows(tn(cot_low, activation), parts).T
    grad_up = reduce_rows(tn(normed2, grad_pre), parts)
    grad_normed2 = nt(grad_pre, up_w)
    grad_residual = cot_low.astype(F32) + normal_back(grad_normed2, gain2, unit2, rate2)
    grad_branch = grad_residual.astype(BF)
    grad_out = reduce_rows(tn(attended, grad_branch), parts)
    grad_attended = nt(grad_branch, out_w).astype(BF)
    heads = (jnp.arange(width)[:, None] // HD == jnp.arange(H)[None]).astype(F32)
    delta = lax.dot_general(
        heads,
        grad_attended.astype(F32) * attended.astype(F32),
        (((0,), (1,)), ((), ())),
        precision=lax.Precision.HIGHEST,
        preferred_element_type=F32,
    )
    results = attend_back(qkv, keys, values, places, grad_attended, lse, delta, bias[:, None])
    if share == 1:
        (grad_qkv,) = results
    else:
        other = lax.psum_scatter(
            jnp.concatenate(results[1:], 1), "core", scatter_dimension=0, tiled=True
        )
        grad_qkv = jnp.concatenate([results[0], other], 1)
    grad_w_qkv = reduce_rows(tn(normed1, grad_qkv), parts)
    grad_normed1 = nt(grad_qkv, qkv_w)
    grad_images = grad_residual + normal_back(grad_normed1, gain1, unit1, rate1)
    grad_images = to_tokens(grad_images.astype(BF))

    def total(field):
        return jnp.sum(field.astype(F32), 0)

    qkv_sums = total(grad_qkv)
    sums = [
        total(grad_normed1 * unit1),
        total(grad_normed1),
        qkv_sums[:width],
        qkv_sums[2 * width :],
        total(grad_branch),
        total(grad_normed2 * unit2),
        total(grad_normed2),
        total(cot_low),
        total(grad_pre),
    ]
    joined = jnp.concatenate([s.reshape(parts, -1) for s in sums], 1)
    joined = lax.psum(joined, ("fsdp",) + SEQ)
    joined = lax.dynamic_index_in_dim(joined, lax.axis_index("fsdp"), 0, keepdims=False)
    small, at = [], 0
    for size in sizes:
        small.append(joined[at : at + size])
        at += size
    g_gain1, g_shift1, g_q, g_v, g_o, g_gain2, g_shift2, g_d, g_u = small
    return (
        layer_out,
        grad_images,
        g_gain1,
        g_shift1,
        grad_w_qkv,
        jnp.stack([g_q, g_v]),
        grad_out,
        g_o,
        g_gain2,
        g_shift2,
        grad_up,
        g_u,
        grad_down,
        g_d,
    )


def solution(mesh):
    fsdp, seq = mesh.shape["fsdp"], mesh.shape["seq"]
    inner = Mesh(mesh.devices.reshape(fsdp, seq // 2, 2), ("fsdp", "z", "core"))
    tokens = P("fsdp", SEQ, None)
    rows, vector, columns = P("fsdp", None), P("fsdp"), P(None, "fsdp")
    return jax.shard_map(
        on_device,
        mesh=inner,
        in_specs=(
            tokens,
            vector,
            vector,
            vector,
            rows,
            columns,
            rows,
            vector,
            vector,
            vector,
            rows,
            vector,
            columns,
            vector,
            tokens,
        ),
        out_specs=(
            tokens,
            tokens,
            vector,
            vector,
            rows,
            columns,
            rows,
            vector,
            vector,
            vector,
            rows,
            vector,
            columns,
            vector,
        ),
        check_vma=False,
    )
```

time: 1680 us -> 1080 us (0.64)
  blocking collectives: 350 us -> 85.3 us
  matrix products: 447 us -> 193 us
  local copies, waits for them, and re-layouts: 242 us -> 106 us
  waiting for transfers between devices: 492 us -> 384 us
  Pallas kernels: 0 us -> 100 us
  starting transfers between devices: 15.5 us -> 58 us
  other arithmetic: 102 us -> 124 us
    all_to_all x1 -> x0, blocking collectives: 277 us -> none  [on_device(): lax.all_to_all(for_sending(grad_stack), 'seq', split_axis=4, concat_axis=...]
    dot_general x125 -> x13, matrix products: 447 us -> 193 us  [the longest x4 80.8 us: nn(): lax.dot_general(a, b, (((1,), (0,)), ((), ())), preferred_element_type=F32)]
    pallas_call x0 -> x2, Pallas kernels: none -> 100 us  [the longest x1 61.4 us: attend_back(): pl.pallas_call(body, grid=(H,), in_specs=[column_block(tokens, 0), column...]
    all_to_all x3 -> x8, waiting for transfers between devices: 286 us -> 205 us  [the longest x4 128 us: reduce_rows(): spread = lax.all_to_all(pair, 'fsdp', 0, 0, tiled=True)]
    ppermute x0 -> x28, waiting for transfers between devices: none -> 56.4 us  [the longest x16 56.3 us: flip(): return lax.ppermute(array, 'fsdp', [(i, i ^ bit) for i in range(4)])]
    while x36 -> x0, local copies, waits for them, and re-layouts: 56.1 us -> none
    all_gather x4 -> x0, waiting for transfers between devices: 55.8 us -> none  [the longest x1 55.8 us: on_device(): lax.all_gather(w_qkv, 'fsdp', axis=0, tiled=True)]
    another operation x5 -> x9, other arithmetic: 9.11 us -> 49.5 us  [the longest x8 48.9 us: gather_rows(): return jnp.stack([first, second], 1).reshape(4 * rows, columns)]
  transfers between devices with their start and end apart: 13 -> 37, of which waited for: 7 -> 12; matrix products, arithmetic and copies ran while one was open for 41% -> 28% of each run, Pallas kernels for 0% -> 4%
where the time goes in v1:
time: 1080 us; the launch traced here: 1070 us
  waiting for transfers between devices  384 us (36%)
  matrix products  193 us (18%)
  other arithmetic  124 us (11%)
  local copies, waits for them, and re-layouts  106 us (10%)
  Pallas kernels  100 us (9%)
  blocking collectives  85.3 us (8%)
  starting transfers between devices  58 us (5%)
  between operations  15.5 us (1%)
    all_to_all x4, waiting for transfers between devices, reduce_rows(): spread = lax.all_to_all(pair, 'fsdp', 0, 0, tiled=True)  128 us
    psum x1, waiting for transfers between devices, reduce_rows(): local = lax.psum(local, 'z')  123 us
    dot_general x4, matrix products, nn(): lax.dot_general(a, b, (((1,), (0,)), ((), ())), preferred_element_type=F32)  80.8 us
    all_to_all x2, waiting for transfers between devices, to_tokens(): lax.all_to_all(field.reshape(seq, piece, width), SEQ, 0, 0, tiled=True)  76.5 us
    pallas_call x1, Pallas kernels, attend_back(): pl.pallas_call(body, grid=(H,), in_specs=[column_block(tokens, 0), column...  61.4 us
    dot_general x4, matrix products, nt(): lax.dot_general(a, b, (((1,), (1,)), ((), ())), preferred_element_type=F32)  60.3 us
    ppermute x16, waiting for transfers between devices, flip(): return lax.ppermute(array, 'fsdp', [(i, i ^ bit) for i in range(4)])  56.3 us
    another operation x8, other arithmetic, gather_rows(): return jnp.stack([first, second], 1).reshape(4 * rows, columns)  48.9 us
  transfers between devices with their start and end apart: 37, of which 12 were waited for; matrix products, arithmetic and copies ran while one was open for 28% of the time, Pallas kernels for 4%

profile of v1, /device:TPU:0, one launch (start us, length us, event | category | flops | bytes accessed | tf_op | source)
XLA Modules:
  0.0 1067.1 jit_solution(17130640606443487908)
XLA Ops:
  31.8 47.9 %all-reduce = bf16[13520]{0:T(1024)(128)(2,1)S(1)} all-reduce(bf16[13520]{0:T(1024)(128)(2,1)S(1)} %dynamic-update-slice), channel_id=2, replica_groups=mesh['fsdp'=4,'z'=4,'core'=2] {'fsdp'}, use_global_device_ids=true, to_apply=%add | all-reduce | flops 13520 | bytes 54080
  99.8 17.1 %collective-permute-done.7 = bf16[72,1152]{1,0:T(8,128)(2,1)S(1)} collective-permute-done((bf16[72,1152]{1,0:T(8,128)(2,1)S(1)}, bf16[72,1152]{1,0:T(8,128)(2,1)S(1)}, u32[]{:S(2)}, u32[]{:S(2)}) %collective-permute-start.7) | collective-permute-done | bytes 165920 | tf_op jit(solution)/shard_map/ppermute | solution.py:220
  138.0 16.4 %collective-permute-done.10 = bf16[144,4304]{1,0:T(8,128)(2,1)S(1)} collective-permute-done((bf16[144,4304]{1,0:T(8,128)(2,1)S(1)}, bf16[144,4304]{1,0:T(8,128)(2,1)S(1)}, u32[]{:S(2)}, u32[]{:S(2)}) %collective-permute-start.10) | collective-permute-done | bytes 1239584 | tf_op jit(solution)/shard_map/ppermute | solution.py:220
  158.3 7.9 collective-permute-done.2
  207.7 15.2 %multiply_convert_fusion.1.q_ref.k_ref.v_ref.refs_0_.refs_1_.refs_2_ = bf16[1024,3456]{1,0:T(8,128)(2,1)} fusion(bf16[1024,1152]{1,0:T(8,128)(2,1)} %bitcast.186, bf16[1152,3456]{1,0:T(8,128)(2,1)} %bitcast.177, f32[3456]{0:T(1024)S(1)} %fusion.63, f32[3456]{0:T(1024)S(1)} %fusion.65), kind=kOutput, calls=%fused_computation.17 | convolution fusion | flops 8164343808 | bytes 17427456 | tf_op jit(solution)/shard_map/dot_general | solution.py:27
  222.9 39.0 %attend.1 = (bf16[1024,1152]{1,0:T(8,128)(2,1)}, f32[16,1024]{1,0:T(8,128)}) custom-call(bf16[1024,3456]{1,0:T(8,128)(2,1)} %multiply_convert_fusion.1.q_ref.k_ref.v_ref.refs_0_.refs_1_.refs_2_, bf16[1024,3456]{1,0:T(8,128)(2,1)} %multiply_convert_fusion.1.q_ref.k_ref.v_ref.refs_0_.refs_1_.refs_2_, ...), custom_call_target="tpu_custom_call" | custom-call | flops 17179869184 | bytes 9437184 | tf_op jit(solution)/shard_map/attend/pallas_call | solution.py:82
  270.8 8.5 select_bitcast_fusion.3
  279.4 8.7 pad_maximum_fusion
  288.0 8.3 copy.31
  296.4 8.5 select_bitcast_fusion.1
  304.9 8.7 pad_maximum_fusion.1
  313.6 25.8 %multiply_convert_fusion = (bf16[1024,4304]{0,1:T(8,128)(2,1)}, f32[1024,4304]{0,1:T(8,128)}) fusion(f32[4304]{0:T(1024)S(1)} %reshape.623, bf16[1152,4304]{1,0:T(8,128)(2,1)} %bitcast.174, f32[1024,1152]{1,0:T(8,128)} %copy-done.2, f32[1152]{0:T(1024)S(1)} %reshape.622, f32[1152]{0:T(1024)S(1)} %reshape.621, f32[1024]{0:T(1024)S(1)} %add_rsqrt_fusion, ...), kind=kOutput, calls=%fused_computation.13 | convolution fusion | flops 10204381184 | bytes 41113408 | tf_op jit(solution)/shard_map/dot_general | solution.py:27
  339.4 33.7 %convert_reduce_fusion = (f32[4304]{0:T(1024)}, bf16[1024,4304]{0,1:T(8,128)(2,1)}) fusion(f32[1024,4304]{0,1:T(8,128)} %get-tuple-element.88, f32[4304]{0:T(1024)S(1)} %reshape.623, bf16[1152,4304]{1,0:T(8,128)(2,1)} %bitcast.172, bf16[1024,1152]{1,0:T(8,128)(2,1)} %bitcast.41), kind=kOutput, calls=%fused_computation.12 | convolution fusion | flops 10260180992 | bytes 38753920 | tf_op jit(solution)/shard_map/dot_general | solution.py:27
  373.1 21.1 %multiply_reduce_fusion = (f32[1152]{0:T(1024)}, f32[1024]{0:T(1024)S(1)}, f32[1024]{0:T(1024)S(1)}, f32[1152]{0:T(1024)}, f32[1024,1152]{1,0:T(8,128)}) fusion(f32[1024,1152]{1,0:T(8,128)} %copy-done.2, f32[1024]{0:T(1024)S(1)} %add_rsqrt_fusion, f32[1024]{0:T(1024)S(1)} %broadcast_multiply_fusion.4, f32[1152]{0:T(1024)S(1)} %reshape.621, ...), kind=kOutput, calls=%fused_computation.62 | convolution fusion | flops 10165022720 | bytes 28198400 | tf_op jit(solution)/shard_map/dot_general | solution.py:23
  394.2 18.6 %convolution_convert_fusion = bf16[1152,4304]{0,1:T(8,128)(2,1)} fusion(bf16[1024,4304]{0,1:T(8,128)(2,1)} %get-tuple-element.92, f32[1024,1152]{1,0:T(8,128)} %copy-done.2, f32[1152]{0:T(1024)S(1)} %reshape.622, f32[1152]{0:T(1024)S(1)} %reshape.621, f32[1024]{0:T(1024)S(1)} %add_rsqrt_fusion, f32[1024]{0:T(1024)S(1)} %broadcast_multiply_fusion.4), kind=kOutput, calls=%fused_computation.2 | convolution fusion | flops 10165266432 | bytes 23467008 | tf_op jit(solution)/shard_map/dot_general | solution.py:31
  424.2 61.4 %attend_back.1 = bf16[1024,3456]{1,0:T(8,128)(2,1)} custom-call(bf16[1024,3456]{1,0:T(8,128)(2,1)} %multiply_convert_fusion.1.q_ref.k_ref.v_ref.refs_0_.refs_1_.refs_2_, bf16[1024,3456]{1,0:T(8,128)(2,1)} %multiply_convert_fusion.1.q_ref.k_ref.v_ref.refs_0_.refs_1_.refs_2_, ...), custom_call_target="tpu_custom_call" | custom-call | flops 42949672960 | bytes 16515072 | tf_op jit(solution)/shard_map/attend_back/pallas_call | solution.py:174
  485.7 16.4 %fusion.29 = (f32[1152]{0:T(1024)S(1)}, f32[1024]{0:T(1024)S(1)}, f32[1024]{0:T(1024)S(1)}, f32[1152]{0:T(1024)S(1)}, bf16[1024,1152]{1,0:T(8,128)(2,1)S(1)}, /*index=5*/f32[1024,1152]{1,0:T(8,128)}) fusion(bf16[8,128,1152]{2,1,0:T(8,128)(2,1)} %copy-done, f32[1024]{0:T(1024)S(1)} %copy-done.23, f32[1024]{0:T(1024)S(1)} %copy-done.24, ...), kind=kOutput, calls=%fused_computation.58 | convolution fusion | flops 8169058304 | bytes 24512512 | tf_op jit(solution)/shard_map/dot_general | solution.py:23
  502.1 9.4 convolution_convert_fusion.2
  521.1 14.1 %copy.33 = bf16[1152,4304]{1,0:T(8,128)(2,1)} copy(bf16[1152,4304]{0,1:T(8,128)(2,1)} %convolution_convert_fusion) | data formatting | bytes 19832832 | tf_op jit(solution)/shard_map/convert_element_type | solution.py:254
  541.9 17.2 %fusion.7 = bf16[1152,4304]{0,1:T(8,128)(2,1)} fusion(bf16[1024,4304]{0,1:T(8,128)(2,1)} %get-tuple-element.87, bf16[1024,1152]{1,0:T(8,128)(2,1)} %bitcast.41), kind=kOutput, calls=%fused_computation.14 | convolution fusion | flops 10159368192 | bytes 21090304 | tf_op jit(solution)/shard_map/dot_general | solution.py:31
  559.1 14.1 %copy.34 = bf16[1152,4304]{1,0:T(8,128)(2,1)} copy(bf16[1152,4304]{0,1:T(8,128)(2,1)} %fusion.7) | data formatting | bytes 19832832 | tf_op jit(solution)/shard_map/convert_element_type | solution.py:254
  579.4 6.2 fusion.10
  585.7 10.8 %all-to-all-done.5 = bf16[4,144,1152]{2,1,0:T(8,128)(2,1)S(1)} async-done(((bf16[4,144,1152]{2,1,0:T(8,128)(2,1)}), bf16[4,144,1152]{2,1,0:T(8,128)(2,1)S(1)}, u32[]{:S(2)}, u32[]{:S(2)}) %all-to-all-start.5) | async-done | bytes 1327136 | tf_op jit(solution)/shard_map/all_to_all | solution.py:258
  606.8 7.4 fusion.9
  614.2 32.3 %all-to-all-done.4 = bf16[4,144,3456]{2,1,0:T(8,128)(2,1)} async-done(((bf16[4,144,3456]{2,1,0:T(8,128)(2,1)}), bf16[4,144,3456]{2,1,0:T(8,128)(2,1)}, u32[]{:S(2)}, u32[]{:S(2)}) %all-to-all-start.4) | async-done | bytes 3981344 | tf_op jit(solution)/shard_map/all_to_all | solution.py:258
  651.6 7.4 fusion.8
  659.0 48.3 %all-to-all-done.6 = bf16[4,144,4304]{2,1,0:T(8,128)(2,1)} async-done(((bf16[4,144,4304]{2,1,0:T(8,128)(2,1)}), bf16[4,144,4304]{2,1,0:T(8,128)(2,1)}, u32[]{:S(2)}, u32[]{:S(2)}) %all-to-all-start.6) | async-done | bytes 4958240 | tf_op jit(solution)/shard_map/all_to_all | solution.py:258
  712.3 18.9 %fusion.36 = bf16[1024,1152]{1,0:T(8,128)(2,1)} fusion(f32[1024,1152]{1,0:T(8,128)} %copy-done.2, bf16[1024,4304]{0,1:T(8,128)(2,1)} %get-tuple-element.87, bf16[1152,4304]{1,0:T(8,128)(2,1)} %bitcast.173, f32[1152]{0:T(1024)S(1)} %reshape.624), kind=kOutput, calls=%fused_computation.78 | convolution fusion | flops 10157948928 | bytes 25813504 | tf_op jit(solution)/shard_map/dot_general | solution.py:23
  731.2 36.8 %all-to-all-done.7 = bf16[4,144,4304]{2,1,0:T(8,128)(2,1)} async-done(((bf16[4,144,4304]{2,1,0:T(8,128)(2,1)}), bf16[4,144,4304]{2,1,0:T(8,128)(2,1)}, u32[]{:S(2)}, u32[]{:S(2)}) %all-to-all-start.7) | async-done | bytes 4958240 | tf_op jit(solution)/shard_map/all_to_all | solution.py:258
  793.5 76.5 %all-to-all-done.1 = bf16[8,128,1152]{2,1,0:T(8,128)(2,1)} async-done(((bf16[8,128,1152]{2,1,0:T(8,128)(2,1)}), bf16[8,128,1152]{2,1,0:T(8,128)(2,1)}, u32[]{:S(2)}, u32[]{:S(2)}) %all-to-all-start.1) | async-done | bytes 2359328 | tf_op jit(solution)/shard_map/all_to_all | solution.py:298
  879.9 123.0 %all-reduce.4.cloned.1.call-done = (bf16[144,3456]{1,0:T(8,128)(2,1)}, bf16[144,1152]{1,0:T(8,128)(2,1)}, bf16[144,4304]{1,0:T(8,128)(2,1)}, bf16[144,4304]{1,0:T(8,128)(2,1)}) async-done(((bf16[144,3456]{1,0:T(8,128)(2,1)}, bf16[144,1152]{1,0:T(8,128)(2,1)}, bf16[144,4304]{1,0:T(8,128)(2,1)}, bf16[144,4304]{1,0:T(8,128)(2,1)}), (bf16[144,3456]{1,0:T(8,128)(2,1)}, bf16[144,1152]{1,0:T(8,128)(2,1)}, ...) | async-done | bytes 3806224 | tf_op jit(solution)/shard_map/psum | solution.py:260
  1003.7 37.4 %psum.35 = f32[4,3380]{1,0:T(4,128)S(1)} all-reduce(f32[4,3380]{1,0:T(4,128)S(1)} %concatenate.23), channel_id=1, replica_groups=mesh['fsdp'=4,'z'=4,'core'=2] {'fsdp','z','core'}, use_global_device_ids=true, to_apply=%region_16.17 | all-reduce | flops 13520 | bytes 108160 | tf_op jit(solution)/shard_map/psum | solution.py:393
  (264 shorter events, 228.5 us)
Async XLA Ops:
  9.6 118.5 %collective-permute-start.15 = (bf16[144,4304]{1,0:T(8,128)(2,1)}, bf16[144,4304]{1,0:T(8,128)(2,1)}, u32[]{:S(2)}, u32[]{:S(2)}) collective-permute-start(bf16[144,4304]{1,0:T(8,128)(2,1)} %dynamic-slice_bitcast_fusion.4), channel_id=1, source_target_pairs={{0,8},{8,0},{16,24},{24,16},{1,9},{9,1},{17,25},{25,17},{2,10},{10... | collective-permute-start | bytes 3718664 | tf_op jit(solution)/shard_map/ppermute | solution.py:220
  12.6 119.2 %collective-permute-start.16 = (bf16[144,4304]{1,0:T(8,128)(2,1)}, bf16[144,4304]{1,0:T(8,128)(2,1)}, u32[]{:S(2)}, u32[]{:S(2)}) collective-permute-start(bf16[144,4304]{1,0:T(8,128)(2,1)} %dynamic-slice_bitcast_fusion.4), channel_id=1, source_target_pairs={{0,16},{8,24},{16,0},{24,8},{1,17},{9,25},{17,1},{25,9},{2,18},{10... | collective-permute-start | bytes 3718664 | tf_op jit(solution)/shard_map/ppermute | solution.py:220
  17.2 75.2 %collective-permute-start.5 = (bf16[144,1152]{1,0:T(8,128)(2,1)}, bf16[144,1152]{1,0:T(8,128)(2,1)}, u32[]{:S(2)}, u32[]{:S(2)}) collective-permute-start(bf16[144,1152]{1,0:T(8,128)(2,1)} %get-tuple-element.43), channel_id=1, source_target_pairs={{0,8},{8,0},{16,24},{24,16},{1,9},{9,1},{17,25},{25,17},{2,10},{10... | collective-permute-start | bytes 995336 | tf_op jit(solution)/shard_map/ppermute | solution.py:220
  17.8 78.7 %collective-permute-start.6 = (bf16[144,1152]{1,0:T(8,128)(2,1)}, bf16[144,1152]{1,0:T(8,128)(2,1)}, u32[]{:S(2)}, u32[]{:S(2)}) collective-permute-start(bf16[144,1152]{1,0:T(8,128)(2,1)} %get-tuple-element.43), channel_id=1, source_target_pairs={{0,16},{8,24},{16,0},{24,8},{1,17},{9,25},{17,1},{25,9},{2,18},{10... | collective-permute-start | bytes 995336 | tf_op jit(solution)/shard_map/ppermute | solution.py:220
  17.8 168.8 %all-to-all-start = ((bf16[8,128,1152]{2,1,0:T(8,128)(2,1)}), bf16[8,128,1152]{2,1,0:T(8,128)(2,1)S(1)}, u32[]{:S(2)}, u32[]{:S(2)}) async-start(bf16[8,128,1152]{2,1,0:T(8,128)(2,1)} %param.15), calls=%async_computation | async-start | bytes 4718592 | tf_op jit(solution)/shard_map/all_to_all | solution.py:294
  28.0 97.1 %collective-permute-start = (bf16[144,3456]{1,0:T(8,128)(2,1)}, bf16[144,3456]{1,0:T(8,128)(2,1)S(1)}, u32[]{:S(2)}, u32[]{:S(2)}) collective-permute-start(bf16[144,3456]{1,0:T(8,128)(2,1)} %get-tuple-element.45), channel_id=1, source_target_pairs={{0,8},{8,0},{16,24},{24,16},{1,9},{9,1},{17,25},{25,17},{2,10},{10... | collective-permute-start | bytes 2985992 | tf_op jit(solution)/shard_map/ppermute | solution.py:220
  92.4 34.6 %collective-permute-start.1 = (bf16[144,3456]{1,0:T(8,128)(2,1)}, bf16[144,3456]{1,0:T(8,128)(2,1)S(1)}, u32[]{:S(2)}, u32[]{:S(2)}) collective-permute-start(bf16[144,3456]{1,0:T(8,128)(2,1)} %get-tuple-element.45), channel_id=1, source_target_pairs={{0,16},{8,24},{16,0},{24,8},{1,17},{9,25},{17,1},{25,9},{2,18},{10... | collective-permute-start | bytes 2985992 | tf_op jit(solution)/shard_map/ppermute | solution.py:220
  96.5 20.3 %collective-permute-start.7 = (bf16[72,1152]{1,0:T(8,128)(2,1)S(1)}, bf16[72,1152]{1,0:T(8,128)(2,1)S(1)}, u32[]{:S(2)}, u32[]{:S(2)}) collective-permute-start(bf16[72,1152]{1,0:T(8,128)(2,1)S(1)} %slice.172), channel_id=1, source_target_pairs={{0,16},{8,24},{16,0},{24,8},{1,17},{9,25},{17,1},{25,9},{2,18},{10... | collective-permute-start | bytes 497672 | tf_op jit(solution)/shard_map/ppermute | solution.py:220
  124.0 30.4 %collective-permute-start.10 = (bf16[144,4304]{1,0:T(8,128)(2,1)S(1)}, bf16[144,4304]{1,0:T(8,128)(2,1)S(1)}, u32[]{:S(2)}, u32[]{:S(2)}) collective-permute-start(bf16[144,4304]{1,0:T(8,128)(2,1)S(1)} %get-tuple-element.41), channel_id=1, source_target_pairs={{0,8},{8,0},{16,24},{24,16},{1,9},{9,1},{17,25},{25,17},{2,10},{10... | collective-permute-start | bytes 3718664 | tf_op jit(solution)/shard_map/ppermute | solution.py:220
  125.1 31.7 %collective-permute-start.11 = (bf16[144,4304]{1,0:T(8,128)(2,1)S(1)}, bf16[144,4304]{1,0:T(8,128)(2,1)S(1)}, u32[]{:S(2)}, u32[]{:S(2)}) collective-permute-start(bf16[144,4304]{1,0:T(8,128)(2,1)S(1)} %get-tuple-element.41), channel_id=1, source_target_pairs={{0,16},{8,24},{16,0},{24,8},{1,17},{9,25},{17,1},{25,9},{2,18},{10... | collective-permute-start | bytes 3718664 | tf_op jit(solution)/shard_map/ppermute | solution.py:220
  127.0 43.7 %collective-permute-start.9 = (bf16[4,144,1152]{2,1,0:T(8,128)(2,1)}, bf16[4,144,1152]{2,1,0:T(8,128)(2,1)S(1)}, u32[]{:S(2)}, u32[]{:S(2)}) collective-permute-start(bf16[4,144,1152]{2,1,0:T(8,128)(2,1)} %bitcast_dynamic-update-slice_fusion.18), channel_id=1, source_target_pairs={{0,1},{1,0},{2,3},{3,2},{4,5},{5,4},{6,7},{7,6},{8,9},{9,8},{10,11... | collective-permute-start | bytes 3981320 | tf_op jit(solution)/shard_map/ppermute | solution.py:224
  128.1 38.1 %collective-permute-start.2 = (bf16[72,3456]{1,0:T(8,128)(2,1)S(1)}, bf16[72,3456]{1,0:T(8,128)(2,1)S(1)}, u32[]{:S(2)}, u32[]{:S(2)}) collective-permute-start(bf16[72,3456]{1,0:T(8,128)(2,1)S(1)} %slice.168), channel_id=1, source_target_pairs={{0,16},{8,24},{16,0},{24,8},{1,17},{9,25},{17,1},{25,9},{2,18},{10... | collective-permute-start | bytes 1493000 | tf_op jit(solution)/shard_map/ppermute | solution.py:220
  131.8 36.1 %collective-permute-start.3 = (bf16[72,3456]{1,0:T(8,128)(2,1)S(1)}, bf16[72,3456]{1,0:T(8,128)(2,1)S(1)}, u32[]{:S(2)}, u32[]{:S(2)}) collective-permute-start(bf16[72,3456]{1,0:T(8,128)(2,1)S(1)} %slice.169), channel_id=1, source_target_pairs={{0,8},{8,0},{16,24},{24,16},{1,9},{9,1},{17,25},{25,17},{2,10},{10... | collective-permute-start | bytes 1493000 | tf_op jit(solution)/shard_map/ppermute | solution.py:220
  154.4 23.8 %collective-permute-start.17 = (bf16[72,4304]{1,0:T(8,128)(2,1)S(1)}, bf16[72,4304]{1,0:T(8,128)(2,1)S(1)}, u32[]{:S(2)}, u32[]{:S(2)}) collective-permute-start(bf16[72,4304]{1,0:T(8,128)(2,1)S(1)} %slice.180), channel_id=1, source_target_pairs={{0,16},{8,24},{16,0},{24,8},{1,17},{9,25},{17,1},{25,9},{2,18},{10... | collective-permute-start | bytes 1859336 | tf_op jit(solution)/shard_map/ppermute | solution.py:220
  156.9 22.2 %collective-permute-start.18 = (bf16[72,4304]{1,0:T(8,128)(2,1)S(1)}, bf16[72,4304]{1,0:T(8,128)(2,1)S(1)}, u32[]{:S(2)}, u32[]{:S(2)}) collective-permute-start(bf16[72,4304]{1,0:T(8,128)(2,1)S(1)} %slice.181), channel_id=1, source_target_pairs={{0,8},{8,0},{16,24},{24,16},{1,9},{9,1},{17,25},{25,17},{2,10},{10... | collective-permute-start | bytes 1859336 | tf_op jit(solution)/shard_map/ppermute | solution.py:220
  166.2 18.7 %collective-permute-start.12 = (bf16[72,4304]{1,0:T(8,128)(2,1)S(1)}, bf16[72,4304]{1,0:T(8,128)(2,1)S(1)}, u32[]{:S(2)}, u32[]{:S(2)}) collective-permute-start(bf16[72,4304]{1,0:T(8,128)(2,1)S(1)} %slice.177), channel_id=1, source_target_pairs={{0,16},{8,24},{16,0},{24,8},{1,17},{9,25},{17,1},{25,9},{2,18},{10... | collective-permute-start | bytes 1859336 | tf_op jit(solution)/shard_map/ppermute | solution.py:220
  170.7 25.9 %collective-permute-start.4 = (bf16[4,144,3456]{2,1,0:T(8,128)(2,1)}, bf16[4,144,3456]{2,1,0:T(8,128)(2,1)}, u32[]{:S(2)}, u32[]{:S(2)}) collective-permute-start(bf16[4,144,3456]{2,1,0:T(8,128)(2,1)} %bitcast_dynamic-update-slice_fusion.13), channel_id=1, source_target_pairs={{0,1},{1,0},{2,3},{3,2},{4,5},{5,4},{6,7},{7,6},{8,9},{9,8},{10,11... | collective-permute-start | bytes 11943944 | tf_op jit(solution)/shard_map/ppermute | solution.py:224
  179.9 116.4 %collective-permute-start.19 = (bf16[4,144,4304]{2,1,0:T(8,128)(2,1)}, bf16[4,144,4304]{2,1,0:T(8,128)(2,1)}, u32[]{:S(2)}, u32[]{:S(2)}) collective-permute-start(bf16[4,144,4304]{2,1,0:T(8,128)(2,1)} %bitcast_dynamic-update-slice_fusion.9), channel_id=1, source_target_pairs={{0,1},{1,0},{2,3},{3,2},{4,5},{5,4},{6,7},{7,6},{8,9},{9,8},{10,11... | collective-permute-start | bytes 14874632 | tf_op jit(solution)/shard_map/ppermute | solution.py:224
  186.6 84.2 %collective-permute-start.14 = (bf16[4,144,4304]{2,1,0:T(8,128)(2,1)}, bf16[4,144,4304]{2,1,0:T(8,128)(2,1)}, u32[]{:S(2)}, u32[]{:S(2)}) collective-permute-start(bf16[4,144,4304]{2,1,0:T(8,128)(2,1)} %bitcast_dynamic-update-slice_fusion.11), channel_id=1, source_target_pairs={{0,1},{1,0},{2,3},{3,2},{4,5},{5,4},{6,7},{7,6},{8,9},{9,8},{10,11... | collective-permute-start | bytes 14874632 | tf_op jit(solution)/shard_map/ppermute | solution.py:224
  186.7 152.8 %all-to-all-start.2 = ((bf16[8,128,1152]{2,1,0:T(8,128)(2,1)}), bf16[8,128,1152]{2,1,0:T(8,128)(2,1)}, u32[]{:S(2)}, u32[]{:S(2)}) async-start(bf16[8,128,1152]{2,1,0:T(8,128)(2,1)} %param.29), calls=%async_computation.2 | async-start | bytes 4718592 | tf_op jit(solution)/shard_map/all_to_all | solution.py:294
  517.3 62.2 %collective-permute-start.20 = (bf16[4,144,3456]{2,1,0:T(8,128)(2,1)}, bf16[4,144,3456]{2,1,0:T(8,128)(2,1)}, u32[]{:S(2)}, u32[]{:S(2)}) collective-permute-start(bf16[4,144,3456]{2,1,0:T(8,128)(2,1)} %dynamic-slice_bitcast_fusion.2), channel_id=1, source_target_pairs={{0,1},{1,0},{2,3},{3,2},{4,5},{5,4},{6,7},{7,6},{8,9},{9,8},{10,11... | collective-permute-start | bytes 11943944 | tf_op jit(solution)/shard_map/ppermute | solution.py:224
  536.4 36.8 %collective-permute-start.22 = (bf16[4,144,1152]{2,1,0:T(8,128)(2,1)}, bf16[4,144,1152]{2,1,0:T(8,128)(2,1)}, u32[]{:S(2)}, u32[]{:S(2)}) collective-permute-start(bf16[4,144,1152]{2,1,0:T(8,128)(2,1)} %dynamic-slice_bitcast_fusion.3), channel_id=1, source_target_pairs={{0,1},{1,0},{2,3},{3,2},{4,5},{5,4},{6,7},{7,6},{8,9},{9,8},{10,11... | collective-permute-start | bytes 3981320 | tf_op jit(solution)/shard_map/ppermute | solution.py:224
  541.4 65.4 %collective-permute-start.24 = (bf16[4,144,4304]{2,1,0:T(8,128)(2,1)}, bf16[4,144,4304]{2,1,0:T(8,128)(2,1)}, u32[]{:S(2)}, u32[]{:S(2)}) collective-permute-start(bf16[4,144,4304]{2,1,0:T(8,128)(2,1)} %dynamic-slice_bitcast_fusion.1), channel_id=1, source_target_pairs={{0,1},{1,0},{2,3},{3,2},{4,5},{5,4},{6,7},{7,6},{8,9},{9,8},{10,11... | collective-permute-start | bytes 14874632 | tf_op jit(solution)/shard_map/ppermute | solution.py:224
  575.9 20.6 %all-to-all-start.5 = ((bf16[4,144,1152]{2,1,0:T(8,128)(2,1)}), bf16[4,144,1152]{2,1,0:T(8,128)(2,1)S(1)}, u32[]{:S(2)}, u32[]{:S(2)}) async-start(bf16[4,144,1152]{2,1,0:T(8,128)(2,1)} %fusion.37), calls=%async_computation.5 | async-start | bytes 2654208 | tf_op jit(solution)/shard_map/all_to_all | solution.py:258
  596.5 50.0 %all-to-all-start.4 = ((bf16[4,144,3456]{2,1,0:T(8,128)(2,1)}), bf16[4,144,3456]{2,1,0:T(8,128)(2,1)}, u32[]{:S(2)}, u32[]{:S(2)}) async-start(bf16[4,144,3456]{2,1,0:T(8,128)(2,1)} %fusion.10), calls=%async_computation.4 | async-start | bytes 7962624 | tf_op jit(solution)/shard_map/all_to_all | solution.py:258
  606.8 44.8 %collective-permute-start.26 = (bf16[4,144,4304]{2,1,0:T(8,128)(2,1)}, bf16[4,144,4304]{2,1,0:T(8,128)(2,1)}, u32[]{:S(2)}, u32[]{:S(2)}) collective-permute-start(bf16[4,144,4304]{2,1,0:T(8,128)(2,1)} %dynamic-slice_bitcast_fusion), channel_id=1, source_target_pairs={{0,1},{1,0},{2,3},{3,2},{4,5},{5,4},{6,7},{7,6},{8,9},{9,8},{10,11... | collective-permute-start | bytes 14874632 | tf_op jit(solution)/shard_map/ppermute | solution.py:224
  646.5 60.8 %all-to-all-start.6 = ((bf16[4,144,4304]{2,1,0:T(8,128)(2,1)}), bf16[4,144,4304]{2,1,0:T(8,128)(2,1)}, u32[]{:S(2)}, u32[]{:S(2)}) async-start(bf16[4,144,4304]{2,1,0:T(8,128)(2,1)} %fusion.9), calls=%async_computation.6 | async-start | bytes 10027008 | tf_op jit(solution)/shard_map/all_to_all | solution.py:258
  707.3 60.7 %all-to-all-start.7 = ((bf16[4,144,4304]{2,1,0:T(8,128)(2,1)}), bf16[4,144,4304]{2,1,0:T(8,128)(2,1)}, u32[]{:S(2)}, u32[]{:S(2)}) async-start(bf16[4,144,4304]{2,1,0:T(8,128)(2,1)} %fusion.8), calls=%async_computation.7 | async-start | bytes 10027008 | tf_op jit(solution)/shard_map/all_to_all | solution.py:258
  768.0 102.1 %all-to-all-start.1 = ((bf16[8,128,1152]{2,1,0:T(8,128)(2,1)}), bf16[8,128,1152]{2,1,0:T(8,128)(2,1)}, u32[]{:S(2)}, u32[]{:S(2)}) async-start(bf16[8,128,1152]{2,1,0:T(8,128)(2,1)} %bitcast.185), calls=%async_computation.1 | async-start | bytes 4718592 | tf_op jit(solution)/shard_map/all_to_all | solution.py:298
  773.4 229.5 %all-reduce.4.cloned.1.call-start = ((), (), s32[]{:S(2)}) async-start(), calls=%async_computation.8 | async-start | bytes 7667712 | tf_op jit(solution)/shard_map/psum | solution.py:260
  870.0 173.1 %all-to-all-start.3 = ((bf16[8,128,1152]{2,1,0:T(8,128)(2,1)}), bf16[8,128,1152]{2,1,0:T(8,128)(2,1)S(1)}, u32[]{:S(2)}, u32[]{:S(2)}) async-start(bf16[8,128,1152]{2,1,0:T(8,128)(2,1)} %bitcast.176), calls=%async_computation.3 | async-start | bytes 4718592 | tf_op jit(solution)/shard_map/all_to_all | solution.py:298
  1002.9 40.7 %collective-permute-start.23 = (bf16[144,1152]{1,0:T(8,128)(2,1)}, bf16[144,1152]{1,0:T(8,128)(2,1)}, u32[]{:S(2)}, u32[]{:S(2)}) collective-permute-start(bf16[144,1152]{1,0:T(8,128)(2,1)} %get-tuple-element.35), channel_id=1, source_target_pairs={{0,1},{1,0},{2,3},{3,2},{4,5},{5,4},{6,7},{7,6},{8,9},{9,8},{10,11... | collective-permute-start | bytes 995336 | tf_op jit(solution)/shard_map/ppermute | solution.py:224
  (46 other events, 1573.7 us)
Sparse Core Ops, SparseCore 0:
  788.0 214.8 all-reduce.3
